TPU v7x, 32 devices: a whole 2x2x4 slice. The times are simulated.
32 devices in a mesh: gx: 8 (over y, x, core), gy: 4 (over z).
Axes of the slice: x: 2, y: 2, z: 4, core: 2. Of those that a mesh axis runs over, the one named last changes fastest.
Arguments:
- populations: float32 [19, 128, 128, 128], P(None, 'gx', 'gy'), may hold values from 0 to 10, as said below
- solid: int32 [128, 128, 128], P('gx', 'gy'), may hold values 0 or 1
Outputs:
- advanced: float32 [19, 128, 128, 128], P(None, 'gx', 'gy')
Inputs may be any that keep to these rules, and one draw needn't show every extreme that they name: populations are positive, each between 0.5 w_i 18 and 1.5 w_i 18.
All inputs are finite; a program needn't handle non-finite values. No bound on the sum of `solid` on one device may be relied on, other than what follows from the above.
Results may differ from a plain program's by a relative error of at most 0.0001.
Values sent between devices are 32-bit elements; how exact they have to be, the bound alone decides.
A program may use at most 128 MiB of HBM per device.

v0:
```python
import functools

import jax
import jax.numpy as jnp
from jax import lax
from jax.experimental import pallas as pl
from jax.experimental.pallas import tpu as pltpu
from jax.sharding import PartitionSpec as P

ITERS = 3
MESH = pl.DeviceIdType.MESH

VELOCITY = (
    (0, 0, 0),
    (1, 0, 0), (-1, 0, 0), (0, 1, 0), (0, -1, 0), (0, 0, 1), (0, 0, -1),
    (1, 1, 0), (-1, -1, 0), (1, -1, 0), (-1, 1, 0),
    (1, 0, 1), (-1, 0, -1), (1, 0, -1), (-1, 0, 1),
    (0, 1, 1), (0, -1, -1), (0, 1, -1), (0, -1, 1),
)
RELAX = 1.6
BIG = 1e37
BLOCKED = 1e34

UP_X = [1, 7, 9, 11, 13]
DOWN_X = [2, 8, 10, 12, 14]
ORDER = UP_X + DOWN_X + [0, 3, 4, 5, 6, 15, 16, 17, 18]
SLOT = {index: slot for slot, index in enumerate(ORDER)}
UP_Y = [3, 7, 10, 15, 17]
DOWN_Y = [4, 8, 9, 16, 18]
CORNERS = (7, 8, 9, 10)


def opposite(index):
    if index == 0:
        return 0
    return index + 1 if index % 2 == 1 else index - 1


def collide(f, fluid):
    total = {}
    delta = {}
    for i in range(1, 19, 2):
        total[i] = f[i] + f[i + 1]
        delta[i] = f[i] - f[i + 1]
    rho = f[0] + ((total[1] + total[3]) + (total[5] + total[7])) + (
        ((total[9] + total[11]) + (total[13] + total[15])) + total[17]
    )
    mx = (delta[1] + delta[7]) + (delta[9] + delta[11]) + delta[13]
    my = (delta[3] + delta[7]) + (delta[15] - delta[9]) + delta[17]
    mz = (delta[5] + delta[11]) + (delta[15] - delta[13]) - delta[17]
    zero = jnp.zeros_like(rho)
    scale = RELAX * 3.0 / 36.0
    mx = jnp.where(fluid, mx * scale, zero)
    my = jnp.where(fluid, my * scale, zero)
    mz = jnp.where(fluid, mz * scale, zero)
    inv = 1.0 / rho
    curve = inv * (RELAX * 4.5 / 36.0 / (scale * scale))
    base = rho * (RELAX / 36.0) - (mx * mx + my * my + mz * mz) * (
        inv * (RELAX * 1.5 / 36.0 / (scale * scale))
    )
    base = jnp.where(fluid, base, jnp.full_like(rho, BIG * RELAX / 36.0))
    post = [None] * 19
    keep = 1.0 - RELAX
    half = keep * 0.5
    post[0] = base * 12.0 + f[0] * keep
    base2 = base + base
    curve2 = curve + curve
    for i in range(1, 19, 2):
        cx, cy, cz = VELOCITY[i]
        along = None
        for c, m in ((cx, mx), (cy, my), (cz, mz)):
            if c == 0:
                continue
            if along is None:
                along = m
            else:
                along = along + m if c > 0 else along - m
        if i < 7:
            even = base2 + along * along * curve2
            odd = along + along
        else:
            even = base + along * along * curve
            odd = along
        even = even + total[i] * half
        odd = odd + delta[i] * half
        post[i] = even + odd
        post[i + 1] = even - odd
    return post


def kernel(sizes, axes, f_hbm, solid_hbm, out, field, solid, p0, p1, p2, y_send, y_recv, in_sem, send_sem, recv_sem):
    rows, cols, gx_size, gy_size = sizes
    gx, gy = axes
    tiles = cols // 8
    buffers = (p0, p1, p2)
    me_x, me_y = lax.axis_index(gx), lax.axis_index(gy)
    up_x, down_x = lax.rem(me_x + 1, gx_size), lax.rem(me_x + gx_size - 1, gx_size)
    up_y, down_y = lax.rem(me_y + 1, gy_size), lax.rem(me_y + gy_size - 1, gy_size)
    place_x = {1: up_x, 0: me_x, -1: down_x}
    place_y = {1: up_y, 0: me_y, -1: down_y}

    def device(dx, dy):
        return {gx: place_x[dx], gy: place_y[dy]}

    inner = rows - 2
    pairs = inner // 2
    half = rows // 2

    def load(start, count, sem):
        return pltpu.make_async_copy(
            f_hbm.at[:, pl.ds(start, count)], field.at[:, pl.ds(start, count)], in_sem.at[sem]
        )

    barrier = pltpu.get_barrier_semaphore()
    around = [(dx, dy) for dx in (-1, 0, 1) for dy in (-1, 0, 1) if (dx, dy) != (0, 0)]
    for dx, dy in around:
        pl.semaphore_signal(barrier, inc=1, device_id=device(dx, dy), device_id_type=MESH)

    load_solid = pltpu.make_async_copy(solid_hbm, solid, in_sem.at[2 + pairs])
    load_solid.start()
    load(0, 1, 0).start()
    load(rows - 1, 1, 1).start()
    for c in range(pairs):
        load(1 + 2 * c, 2, 2 + c).start()

    def remote(src, dst, phase, which, dx, dy):
        return pltpu.make_async_remote_copy(
            src_ref=src,
            dst_ref=dst,
            send_sem=send_sem.at[phase, which],
            recv_sem=recv_sem.at[phase, which],
            device_id=device(dx, dy),
            device_id_type=MESH,
        )

    def x_copies(phase, side):
        buf = buffers[phase]
        own = pl.ds(8, cols)
        src_x, dst_x, slots = (rows, 0, pl.ds(0, 5)) if side > 0 else (1, rows + 1, pl.ds(5, 5))
        copies = [
            remote(
                buf.at[slots, src_x, own], buf.at[slots, dst_x, own], phase, 0 if side > 0 else 1, side, 0
            )
        ]
        for k, index in enumerate(CORNERS):
            cx, cy, _ = VELOCITY[index]
            if cx != side:
                continue
            slot = SLOT[index]
            src_y, dst_y = (cols, 0) if cy > 0 else (8, cols + 8)
            copies.append(
                remote(
                    buf.at[slot, src_x, pl.ds(src_y, 8)],
                    buf.at[slot, dst_x, pl.ds(dst_y, 8)],
                    phase, 2 + k, cx, cy,
                )
            )
        return copies

    def y_copies(phase, chunk):
        planes = pl.ds(chunk * half, half)
        return [
            remote(
                y_send.at[phase, side, :, planes], y_recv.at[phase, side, :, planes],
                phase, 6 + 2 * side + chunk, 0, 1 - 2 * side,
            )
            for side in range(2)
        ]

    def pull(buf, x, t):
        top = 8 + 8 * t
        own = [buf[SLOT[i], x + 1, pl.ds(top, 8), :] for i in range(19)]
        f = [own[0]]
        for i in range(1, 19):
            cx, cy, cz = VELOCITY[i]
            if cx == 0 and cy == 0:
                value = own[i]
            else:
                value = buf[SLOT[i], x + 1 - cx, pl.ds(top - cy, 8), :]
            if cz:
                value = pltpu.roll(value, 1 if cz > 0 else value.shape[1] - 1, axis=1)
            f.append(jnp.where(value > BLOCKED, own[opposite(i)], value))
        return f

    def advance(phase, x, t):
        fluid = solid[x, pl.ds(8 * t, 8), :] == 0
        if phase == 0:
            f = [field[i, x, pl.ds(8 * t, 8), :] for i in range(19)]
        else:
            f = pull(buffers[phase - 1], x, t)
        post = collide(f, fluid)
        buf = buffers[phase]
        for i in range(19):
            buf[SLOT[i], x + 1, pl.ds(8 + 8 * t, 8), :] = post[i]
        if t == tiles - 1:
            for j, index in enumerate(UP_Y):
                y_send[phase, 0, j, pl.ds(x, 1), :] = post[index][7:8]
        if t == 0:
            for j, index in enumerate(DOWN_Y):
                y_send[phase, 1, j, pl.ds(x, 1), :] = post[index][0:1]

    def finish(x, t):
        fluid = solid[x, pl.ds(8 * t, 8), :] == 0
        f = pull(buffers[ITERS - 1], x, t)
        for i in range(19):
            kept = field[i, x, pl.ds(8 * t, 8), :]
            out[i, x, pl.ds(8 * t, 8), :] = jnp.where(fluid, f[i], kept)

    edge_tiles = sorted({0, tiles - 1})
    inner_tiles = [t for t in range(tiles) if t not in edge_tiles]

    def loop(body, which, first=1, stop=rows - 1):
        if not which:
            return

        def step(c, carry):
            for dx in range(2):
                for t in which:
                    body(first + 2 * c + dx, t)
            return carry

        lax.fori_loop(0, (stop - first) // 2, step, 0)

    def merge(phase, chunk):
        buf = buffers[phase]

        def step(c, carry):
            for dx in range(2):
                x = chunk * half + 2 * c + dx
                for j, index in enumerate(UP_Y):
                    buf[SLOT[index], x + 1, pl.ds(7, 1), :] = y_recv[phase, 0, j, pl.ds(x, 1), :]
                for j, index in enumerate(DOWN_Y):
                    buf[SLOT[index], x + 1, pl.ds(cols + 8, 1), :] = y_recv[phase, 1, j, pl.ds(x, 1), :]
            return carry

        lax.fori_loop(0, half // 2, step, 0)

    def plane(body, x):
        for t in range(tiles):
            body(x, t)

    def arrive(copies):
        for copy in copies:
            copy.wait_recv()

    def send(copies):
        for copy in copies:
            copy.start()

    first_pairs = (half - 2) // 2

    def loaded(low, high):
        for c in range(low, high):
            load(1 + 2 * c, 2, 2 + c).wait()

    for phase in range(ITERS):
        body = functools.partial(advance, phase)
        if phase == 0:
            load_solid.wait()
            load(0, 1, 0).wait()
            plane(body, 0)
            pl.semaphore_wait(barrier, len(around))
            send(x_copies(phase, -1))
            load(rows - 1, 1, 1).wait()
            plane(body, rows - 1)
            send(x_copies(phase, 1))
            loaded(0, first_pairs)
            loop(body, edge_tiles, 1, half - 1)
            loaded(first_pairs, first_pairs + 1)
        else:
            arrive(y_copies(phase - 1, 0))
            merge(phase - 1, 0)
            arrive(x_copies(phase - 1, 1))
            plane(body, 0)
            send(x_copies(phase, -1))
            loop(body, edge_tiles, 1, half - 1)
            arrive(y_copies(phase - 1, 1))
            merge(phase - 1, 1)
            arrive(x_copies(phase - 1, -1))
            plane(body, rows - 1)
            send(x_copies(phase, 1))
        loop(body, edge_tiles, half - 1, half + 1)
        send(y_copies(phase, 0))
        if phase == 0:
            loaded(first_pairs + 1, pairs)
        loop(body, edge_tiles, half + 1, rows - 1)
        send(y_copies(phase, 1))
        loop(body, inner_tiles)

    last = ITERS - 1
    loop(finish, inner_tiles)
    arrive(y_copies(last, 0))
    merge(last, 0)
    arrive(x_copies(last, 1))
    plane(finish, 0)
    loop(finish, edge_tiles, 1, half - 1)
    arrive(y_copies(last, 1))
    merge(last, 1)
    loop(finish, edge_tiles, half - 1, rows - 1)
    arrive(x_copies(last, -1))
    plane(finish, rows - 1)
    for phase in range(ITERS):
        for copy in x_copies(phase, 1) + x_copies(phase, -1) + y_copies(phase, 0) + y_copies(phase, 1):
            copy.wait_send()


def solution(mesh):
    gx, gy = mesh.axis_names
    gx_size, gy_size = mesh.shape[gx], mesh.shape[gy]

    def local(populations, solid):
        count, rows, cols, lanes = populations.shape
        f32 = jnp.float32
        padded = pltpu.VMEM((count, rows + 2, cols + 16, lanes), f32)
        return pl.pallas_call(
            functools.partial(kernel, (rows, cols, gx_size, gy_size), (gx, gy)),
            out_shape=jax.ShapeDtypeStruct(populations.shape, f32),
            in_specs=[pl.BlockSpec(memory_space=pltpu.HBM)] * 2,
            out_specs=pl.BlockSpec(memory_space=pltpu.VMEM),
            scratch_shapes=[
                pltpu.VMEM((count, rows, cols, lanes), f32),
                pltpu.VMEM((rows, cols, lanes), jnp.int32),
                padded,
                padded,
                padded,
                pltpu.VMEM((ITERS, 2, 5, rows, lanes), f32),
                pltpu.VMEM((ITERS, 2, 5, rows, lanes), f32),
                pltpu.SemaphoreType.DMA((3 + (rows - 2) // 2,)),
                pltpu.SemaphoreType.DMA((ITERS, 10)),
                pltpu.SemaphoreType.DMA((ITERS, 10)),
            ],
            compiler_params=pltpu.CompilerParams(
                collective_id=0, has_side_effects=True, vmem_limit_bytes=46 * 1024 * 1024
            ),
        )(
            pltpu.with_memory_space_constraint(populations, pltpu.HBM),
            pltpu.with_memory_space_constraint(solid, pltpu.HBM),
        )

    return jax.shard_map(
        local,
        mesh=mesh,
        in_specs=(P(None, gx, gy, None), P(gx, gy, None)),
        out_specs=P(None, gx, gy, None),
        check_vma=False,
    )
```

profile of v0, /device:TPU:0, one launch (start us, length us, event | category | flops | bytes accessed | tf_op | source)
XLA Modules:
  0.0 24.0 jit_solution(2183658976167638483)
XLA Ops:
  0.0 21.7 %shard_map.28 = f32[19,16,32,128]{3,2,1,0:T(8,128)S(1)} custom-call(f32[19,16,32,128]{3,2,1,0:T(8,128)} %f_hbm.1, s32[16,32,128]{2,1,0:T(8,128)} %solid_hbm.1), custom_call_target="tpu_custom_call" | custom-call | tf_op jit(solution)/shard_map/pallas_call | solution.py:315
  21.7 2.3 %copy.4 = f32[19,16,32,128]{3,2,1,0:T(8,128)} copy(f32[19,16,32,128]{3,2,1,0:T(8,128)S(1)} %shard_map.28) | data formatting | bytes 9961472
where the time goes:
time: 24.2 us; the launch traced here: 24 us
  Pallas kernels  21.7 us (90%)
  local copies, waits for them, and re-layouts  2.27 us (9%)
    pallas_call x1, Pallas kernels, local(): pl.pallas_call(functools.partial(kernel, (rows, cols, gx_size, gy_size),...  21.7 us
    unnamed x1, local copies, waits for them, and re-layouts  2.27 us

commit v1 on v0

v1 whole, which is shorter than its diff:
```python
import functools

import jax
import jax.numpy as jnp
from jax import lax
from jax.experimental import pallas as pl
from jax.experimental.pallas import tpu as pltpu
from jax.sharding import PartitionSpec as P

ITERS = 3
MESH = pl.DeviceIdType.MESH

VELOCITY = (
    (0, 0, 0),
    (1, 0, 0), (-1, 0, 0), (0, 1, 0), (0, -1, 0), (0, 0, 1), (0, 0, -1),
    (1, 1, 0), (-1, -1, 0), (1, -1, 0), (-1, 1, 0),
    (1, 0, 1), (-1, 0, -1), (1, 0, -1), (-1, 0, 1),
    (0, 1, 1), (0, -1, -1), (0, 1, -1), (0, -1, 1),
)
RELAX = 1.6
BIG = 1e37
BLOCKED = 1e34

ORDER = [9, 1, 11, 13, 7, 3, 15, 17, 10, 2, 12, 14, 8, 4, 16, 18, 0, 5, 6]
SLOT = {index: slot for slot, index in enumerate(ORDER)}
UP_Y = [7, 3, 15, 17, 10]
DOWN_Y = [8, 4, 16, 18, 9]
CORNERS = (7, 8, 9, 10)
PAD = 8


def opposite(index):
    if index == 0:
        return 0
    return index + 1 if index % 2 == 1 else index - 1


def collide(f, fluid, wanted=range(19)):
    total = {}
    delta = {}
    for i in range(1, 19, 2):
        total[i] = f[i] + f[i + 1]
        delta[i] = f[i] - f[i + 1]
    rho = f[0] + ((total[1] + total[3]) + (total[5] + total[7])) + (
        ((total[9] + total[11]) + (total[13] + total[15])) + total[17]
    )
    mx = (delta[1] + delta[7]) + (delta[9] + delta[11]) + delta[13]
    my = (delta[3] + delta[7]) + (delta[15] - delta[9]) + delta[17]
    mz = (delta[5] + delta[11]) + (delta[15] - delta[13]) - delta[17]
    zero = jnp.zeros_like(rho)
    scale = RELAX * 3.0 / 36.0
    mx = jnp.where(fluid, mx * scale, zero)
    my = jnp.where(fluid, my * scale, zero)
    mz = jnp.where(fluid, mz * scale, zero)
    inv = 1.0 / rho
    curve = inv * (RELAX * 4.5 / 36.0 / (scale * scale))
    base = rho * (RELAX / 36.0) - (mx * mx + my * my + mz * mz) * (
        inv * (RELAX * 1.5 / 36.0 / (scale * scale))
    )
    base = jnp.where(fluid, base, jnp.full_like(rho, BIG * RELAX / 36.0))
    post = [None] * 19
    keep = 1.0 - RELAX
    half = keep * 0.5
    if 0 in wanted:
        post[0] = base * 12.0 + f[0] * keep
    base2 = base + base
    curve2 = curve + curve
    for i in range(1, 19, 2):
        if i not in wanted and i + 1 not in wanted:
            continue
        cx, cy, cz = VELOCITY[i]
        along = None
        for c, m in ((cx, mx), (cy, my), (cz, mz)):
            if c == 0:
                continue
            if along is None:
                along = m
            else:
                along = along + m if c > 0 else along - m
        if i < 7:
            even = base2 + along * along * curve2
            odd = along + along
        else:
            even = base + along * along * curve
            odd = along
        even = even + total[i] * half
        odd = odd + delta[i] * half
        if i in wanted:
            post[i] = even + odd
        if i + 1 in wanted:
            post[i + 1] = even - odd
    return post


def pull(load):
    own = [load(SLOT[i], 0, 0) for i in range(19)]
    f = [own[0]]
    for i in range(1, 19):
        cx, cy, cz = VELOCITY[i]
        value = own[i] if cx == 0 and cy == 0 else load(SLOT[i], cx, cy)
        if cz:
            value = pltpu.roll(value, 1 if cz > 0 else value.shape[1] - 1, axis=1)
        f.append(jnp.where(value > BLOCKED, own[opposite(i)], value))
    return f


def flatten(buf):
    count, planes, pitch, lanes = buf.shape
    return buf.reshape(count, planes * pitch, lanes)


def tile_load(buf, x, t):
    pitch = buf.shape[2]
    view = flatten(buf)

    def load(slot, cx, cy):
        first = PAD + 8 * t - cy
        if first + 8 > pitch:
            return view[slot, pl.ds((x + 1 - cx) * pitch + first, 8), :]
        return buf[slot, x + 1 - cx, pl.ds(first, 8), :]

    return load


def step_kernel(sizes, axes, f_hbm, solid_hbm, p2, field, solid, p0, p1, f_row, s_row, y_send, in_sem, send_sem, recv_sem):
    rows, cols, gx_size, gy_size = sizes
    gx, gy = axes
    tiles = cols // 8
    pitch = cols + PAD
    buffers = (p0, p1, p2)
    flat = [flatten(buf) for buf in buffers]
    me_x, me_y = lax.axis_index(gx), lax.axis_index(gy)
    up_x, down_x = lax.rem(me_x + 1, gx_size), lax.rem(me_x + gx_size - 1, gx_size)
    up_y, down_y = lax.rem(me_y + 1, gy_size), lax.rem(me_y + gy_size - 1, gy_size)
    place_x = {1: up_x, 0: me_x, -1: down_x}
    place_y = {1: up_y, 0: me_y, -1: down_y}

    def device(dx, dy):
        return {gx: place_x[dx], gy: place_y[dy]}

    pairs = (rows - 2) // 2
    edge_y = (cols - 1, 0)

    def load(start, count, sem):
        return pltpu.make_async_copy(
            f_hbm.at[:, pl.ds(start, count)], field.at[:, pl.ds(start, count)], in_sem.at[sem]
        )

    barrier = pltpu.get_barrier_semaphore()
    around = [(dx, dy) for dx in (-1, 0, 1) for dy in (-1, 0, 1) if (dx, dy) != (0, 0)]
    for dx, dy in around:
        pl.semaphore_signal(barrier, inc=1, device_id=device(dx, dy), device_id_type=MESH)

    row_loads = []
    for side, y in enumerate(edge_y):
        row_loads.append(pltpu.make_async_copy(f_hbm.at[:, :, y], f_row.at[side], in_sem.at[2 * side]))
        row_loads.append(pltpu.make_async_copy(solid_hbm.at[:, y], s_row.at[side], in_sem.at[2 * side + 1]))
    for copy in row_loads:
        copy.start()
    load_solid = pltpu.make_async_copy(solid_hbm, solid, in_sem.at[4])
    load_solid.start()
    ends = [load(0, 1, 5), load(rows - 1, 1, 6)]
    inner = [load(1 + 2 * c, 2, 7 + c) for c in range(pairs)]
    for copy in ends + inner:
        copy.start()

    def remote(src, dst, phase, which, dx, dy):
        return pltpu.make_async_remote_copy(
            src_ref=src,
            dst_ref=dst,
            send_sem=send_sem.at[phase, which],
            recv_sem=recv_sem.at[phase, which],
            device_id=device(dx, dy),
            device_id_type=MESH,
        )

    def x_copies(phase):
        buf = buffers[phase]
        own = pl.ds(PAD, cols)
        up, down = pl.ds(0, 5), pl.ds(8, 5)
        return [
            remote(buf.at[up, rows, own], buf.at[up, 0, own], phase, 0, 1, 0),
            remote(buf.at[down, 1, own], buf.at[down, rows + 1, own], phase, 1, -1, 0),
        ]

    def corner_copies(phase):
        buf = buffers[phase]
        copies = []
        for k, index in enumerate(CORNERS):
            cx, cy, _ = VELOCITY[index]
            side = 0 if cy > 0 else 1
            j = (UP_Y, DOWN_Y)[side].index(index)
            src_x, dst_x = (rows - 1, 0) if cx > 0 else (0, rows + 1)
            dst = buf.at[SLOT[index], dst_x, PAD - 1] if cy > 0 else buf.at[SLOT[index], dst_x + 1, 0]
            copies.append(remote(y_send.at[phase, side, j, src_x], dst, phase, 2 + k, cx, cy))
        return copies

    def y_copies(phase):
        buf = buffers[phase]
        return [
            remote(y_send.at[phase, 0], buf.at[pl.ds(4, 5), pl.ds(1, rows), PAD - 1], phase, 6, 0, 1),
            remote(y_send.at[phase, 1, pl.ds(0, 4)], buf.at[pl.ds(12, 4), pl.ds(2, rows), 0], phase, 7, 0, -1),
            remote(y_send.at[phase, 1, 4], buf.at[0, pl.ds(2, rows), 0], phase, 8, 0, -1),
        ]

    def row(phase, side, g):
        fluid = s_row[side, pl.ds(8 * g, 8), :] == 0
        if phase == 0:
            f = [f_row[side, i, pl.ds(8 * g, 8), :] for i in range(19)]
        else:
            view = flat[phase - 1]

            def strided(slot, cx, cy):
                start = (8 * g + 1 - cx) * pitch + PAD + edge_y[side] - cy
                return view[slot, pl.ds(start, 8, stride=pitch), :]

            f = pull(strided)
        wanted = (UP_Y, DOWN_Y)[side]
        post = collide(f, fluid, wanted)
        for j, index in enumerate(wanted):
            y_send[phase, side, j, pl.ds(8 * g, 8), :] = post[index]

    def advance(phase, x, t):
        fluid = solid[x, pl.ds(8 * t, 8), :] == 0
        if phase == 0:
            f = [field[i, x, pl.ds(8 * t, 8), :] for i in range(19)]
        else:
            f = pull(tile_load(buffers[phase - 1], x, t))
        post = collide(f, fluid)
        for i in range(19):
            buffers[phase][SLOT[i], x + 1, pl.ds(PAD + 8 * t, 8), :] = post[i]

    def plane(phase, x):
        for t in range(tiles):
            advance(phase, x, t)

    def start(copies):
        for copy in copies:
            copy.start()

    for phase in range(ITERS):
        if phase == 0:
            for copy in row_loads:
                copy.wait()
        else:
            for copy in x_copies(phase - 1) + y_copies(phase - 1) + corner_copies(phase - 1):
                copy.wait_recv()
        for side in range(2):
            for g in range(rows // 8):
                row(phase, side, g)
        if phase == 0:
            pl.semaphore_wait(barrier, len(around))
        start(corner_copies(phase))
        start(y_copies(phase))
        if phase == 0:
            load_solid.wait()
            for copy in ends:
                copy.wait()
        plane(phase, rows - 1)
        plane(phase, 0)
        start(x_copies(phase))
        if phase == 0:
            for copy in inner:
                copy.wait()

        def step(x, carry):
            plane(phase, x)
            return carry

        lax.fori_loop(1, rows - 1, step, 0)

    last = ITERS - 1
    for copy in x_copies(last) + y_copies(last) + corner_copies(last):
        copy.wait_recv()
    for phase in range(ITERS):
        for copy in x_copies(phase) + y_copies(phase) + corner_copies(phase):
            copy.wait_send()


def finish_kernel(buf, field, out, stage, sem):
    count, rows, cols, _ = stage.shape

    def copy(x):
        return pltpu.make_async_copy(stage.at[:, x], out.at[:, x], sem.at[x])

    def step(x, carry):
        for t in range(cols // 8):
            load = tile_load(buf, x, t)
            f = pull(load)
            fluid = f[0] < BLOCKED
            for i in range(count):
                kept = field[i, x, pl.ds(8 * t, 8), :]
                stage[i, x, pl.ds(8 * t, 8), :] = jnp.where(fluid, f[i], kept)
        copy(x).start()
        return carry

    lax.fori_loop(0, rows, step, 0)
    for x in range(rows):
        copy(x).wait()


def solution(mesh):
    gx, gy = mesh.axis_names
    gx_size, gy_size = mesh.shape[gx], mesh.shape[gy]

    def local(populations, solid):
        count, rows, cols, lanes = populations.shape
        f32 = jnp.float32
        padded = (count, rows + 3, cols + PAD, lanes)
        vmem = pl.BlockSpec(memory_space=pltpu.VMEM)
        hbm = pl.BlockSpec(memory_space=pltpu.HBM)
        post, field = pl.pallas_call(
            functools.partial(step_kernel, (rows, cols, gx_size, gy_size), (gx, gy)),
            out_shape=(
                jax.ShapeDtypeStruct(padded, f32),
                jax.ShapeDtypeStruct(populations.shape, f32),
            ),
            in_specs=[hbm, hbm],
            out_specs=(vmem, vmem),
            scratch_shapes=[
                pltpu.VMEM((rows, cols, lanes), jnp.int32),
                pltpu.VMEM(padded, f32),
                pltpu.VMEM(padded, f32),
                pltpu.VMEM((2, count, rows, lanes), f32),
                pltpu.VMEM((2, rows, lanes), jnp.int32),
                pltpu.VMEM((ITERS, 2, 5, rows, lanes), f32),
                pltpu.SemaphoreType.DMA((7 + (rows - 2) // 2,)),
                pltpu.SemaphoreType.DMA((ITERS, 9)),
                pltpu.SemaphoreType.DMA((ITERS, 9)),
            ],
            compiler_params=pltpu.CompilerParams(
                collective_id=0, has_side_effects=True, vmem_limit_bytes=30 * 1024 * 1024
            ),
        )(
            pltpu.with_memory_space_constraint(populations, pltpu.HBM),
            pltpu.with_memory_space_constraint(solid, pltpu.HBM),
        )
        return pl.pallas_call(
            finish_kernel,
            out_shape=jax.ShapeDtypeStruct(populations.shape, f32),
            in_specs=[vmem, vmem],
            out_specs=hbm,
            scratch_shapes=[
                pltpu.VMEM(populations.shape, f32),
                pltpu.SemaphoreType.DMA((rows,)),
            ],
            compiler_params=pltpu.CompilerParams(vmem_limit_bytes=12 * 1024 * 1024),
        )(post, field)

    return jax.shard_map(
        local,
        mesh=mesh,
        in_specs=(P(None, gx, gy, None), P(gx, gy, None)),
        out_specs=P(None, gx, gy, None),
        check_vma=False,
    )
```

time: 24.2 us -> 22.7 us (0.938)
  local copies, waits for them, and re-layouts: 2.27 us -> 0 us
  Pallas kernels: 21.7 us -> 22.6 us
    unnamed x1 -> x0, local copies, waits for them, and re-layouts: 2.27 us -> none
    pallas_call x1 -> x2, Pallas kernels: 21.7 us -> 22.6 us  [the longest x1 19.8 us: local(): pl.pallas_call(functools.partial(step_kernel, (rows, cols, gx_size, gy_si...]
where the time goes in v1:
time: 22.7 us; the launch traced here: 22.6 us
  Pallas kernels  22.6 us (100%)
    pallas_call x1, Pallas kernels, local(): pl.pallas_call(functools.partial(step_kernel, (rows, cols, gx_size, gy_si...  19.8 us
    pallas_call x1, Pallas kernels, local(): pl.pallas_call(finish_kernel, out_shape=jax.ShapeDtypeStruct(populations....  2.76 us

profile of v1, /device:TPU:0, one launch (start us, length us, event | category | flops | bytes accessed | tf_op | source)
XLA Modules:
  0.0 22.6 jit_solution(11682291706132433148)
XLA Ops:
  0.0 19.8 %shard_map.28 = (f32[19,19,40,128]{3,2,1,0:T(8,128)S(1)}, f32[19,16,32,128]{3,2,1,0:T(8,128)S(1)}) custom-call(f32[19,16,32,128]{3,2,1,0:T(8,128)} %f_hbm.1, s32[16,32,128]{2,1,0:T(8,128)} %solid_hbm.1), custom_call_target="tpu_custom_call" | custom-call | tf_op jit(solution)/shard_map/pallas_call | solution.py:312
  19.8 2.8 %shard_map.29 = f32[19,16,32,128]{3,2,1,0:T(8,128)} custom-call(f32[19,19,40,128]{3,2,1,0:T(8,128)S(1)} %get-tuple-element.7.buf, f32[19,16,32,128]{3,2,1,0:T(8,128)S(1)} %get-tuple-element.8.field), custom_call_target="tpu_custom_call" | custom-call | tf_op jit(solution)/shard_map/pallas_call | solution.py:338

commit v2 on v1

--- a/solution.py
+++ b/solution.py
@@ -127,6 +127,7 @@
     gx, gy = axes
     tiles = cols // 8
     pitch = cols + PAD
+    sent = 10 * (rows + cols) + len(CORNERS)
     buffers = (p0, p1, p2)
     flat = [flatten(buf) for buf in buffers]
     me_x, me_y = lax.axis_index(gx), lax.axis_index(gy)
@@ -142,8 +143,9 @@
     edge_y = (cols - 1, 0)
 
     def load(start, count, sem):
+        planes = pl.ds(start, count)
         return pltpu.make_async_copy(
-            f_hbm.at[:, pl.ds(start, count)], field.at[:, pl.ds(start, count)], in_sem.at[sem]
+            f_hbm.at[:, planes], field.at[:, planes, pl.ds(0, cols)], in_sem.at[sem]
         )
 
     barrier = pltpu.get_barrier_semaphore()
@@ -153,23 +155,26 @@
 
     row_loads = []
     for side, y in enumerate(edge_y):
-        row_loads.append(pltpu.make_async_copy(f_hbm.at[:, :, y], f_row.at[side], in_sem.at[2 * side]))
-        row_loads.append(pltpu.make_async_copy(solid_hbm.at[:, y], s_row.at[side], in_sem.at[2 * side + 1]))
-    for copy in row_loads:
+        row_loads.append(pltpu.make_async_copy(f_hbm.at[:, :, y], f_row.at[side], in_sem.at[0]))
+        row_loads.append(pltpu.make_async_copy(solid_hbm.at[:, y], s_row.at[side], in_sem.at[1 + side]))
+    load_solid = pltpu.make_async_copy(solid_hbm, solid, in_sem.at[3])
+    ends = [load(0, 1, 4), load(rows - 1, 1, 4)]
+    inner = [load(1 + 2 * c, 2, 5) for c in range(pairs)]
+    for copy in row_loads + [load_solid] + ends + inner:
         copy.start()
-    load_solid = pltpu.make_async_copy(solid_hbm, solid, in_sem.at[4])
-    load_solid.start()
-    ends = [load(0, 1, 5), load(rows - 1, 1, 6)]
-    inner = [load(1 + 2 * c, 2, 7 + c) for c in range(pairs)]
-    for copy in ends + inner:
-        copy.start()
-
-    def remote(src, dst, phase, which, dx, dy):
+
+    def wait_rows():
+        both = (slice(None), pl.ds(0, 2), pl.ds(0, rows))
+        pltpu.make_async_copy(f_hbm.at[both], field.at[both], in_sem.at[0]).wait()
+        row_loads[1].wait()
+        row_loads[3].wait()
+
+    def remote(src, dst, phase, dx, dy):
         return pltpu.make_async_remote_copy(
             src_ref=src,
             dst_ref=dst,
-            send_sem=send_sem.at[phase, which],
-            recv_sem=recv_sem.at[phase, which],
+            send_sem=send_sem.at[0],
+            recv_sem=recv_sem.at[phase],
             device_id=device(dx, dy),
             device_id_type=MESH,
         )
@@ -179,29 +184,33 @@
         own = pl.ds(PAD, cols)
         up, down = pl.ds(0, 5), pl.ds(8, 5)
         return [
-            remote(buf.at[up, rows, own], buf.at[up, 0, own], phase, 0, 1, 0),
-            remote(buf.at[down, 1, own], buf.at[down, rows + 1, own], phase, 1, -1, 0),
+            remote(buf.at[up, rows, own], buf.at[up, 0, own], phase, 1, 0),
+            remote(buf.at[down, 1, own], buf.at[down, rows + 1, own], phase, -1, 0),
         ]
 
     def corner_copies(phase):
         buf = buffers[phase]
         copies = []
-        for k, index in enumerate(CORNERS):
+        for index in CORNERS:
             cx, cy, _ = VELOCITY[index]
             side = 0 if cy > 0 else 1
             j = (UP_Y, DOWN_Y)[side].index(index)
             src_x, dst_x = (rows - 1, 0) if cx > 0 else (0, rows + 1)
             dst = buf.at[SLOT[index], dst_x, PAD - 1] if cy > 0 else buf.at[SLOT[index], dst_x + 1, 0]
-            copies.append(remote(y_send.at[phase, side, j, src_x], dst, phase, 2 + k, cx, cy))
+            copies.append(remote(y_send.at[phase, side, j, src_x], dst, phase, cx, cy))
         return copies
 
     def y_copies(phase):
         buf = buffers[phase]
         return [
-            remote(y_send.at[phase, 0], buf.at[pl.ds(4, 5), pl.ds(1, rows), PAD - 1], phase, 6, 0, 1),
-            remote(y_send.at[phase, 1, pl.ds(0, 4)], buf.at[pl.ds(12, 4), pl.ds(2, rows), 0], phase, 7, 0, -1),
-            remote(y_send.at[phase, 1, 4], buf.at[0, pl.ds(2, rows), 0], phase, 8, 0, -1),
+            remote(y_send.at[phase, 0], buf.at[pl.ds(4, 5), pl.ds(1, rows), PAD - 1], phase, 0, 1),
+            remote(y_send.at[phase, 1, pl.ds(0, 4)], buf.at[pl.ds(12, 4), pl.ds(2, rows), 0], phase, 0, -1),
+            remote(y_send.at[phase, 1, 4], buf.at[0, pl.ds(2, rows), 0], phase, 0, -1),
         ]
+
+    def arrive(phase):
+        view = flat[phase].at[0, pl.ds(0, sent)]
+        remote(view, view, phase, 1, 0).wait_recv()
 
     def row(phase, side, g):
         fluid = s_row[side, pl.ds(8 * g, 8), :] == 0
@@ -238,30 +247,57 @@
         for copy in copies:
             copy.start()
 
-    for phase in range(ITERS):
-        if phase == 0:
-            for copy in row_loads:
-                copy.wait()
-        else:
-            for copy in x_copies(phase - 1) + y_copies(phase - 1) + corner_copies(phase - 1):
-                copy.wait_recv()
+    def edge_rows(phase):
         for side in range(2):
             for g in range(rows // 8):
                 row(phase, side, g)
+
+    def finish(x, t):
+        f = pull(tile_load(p2, x, t))
+        fluid = f[0] < BLOCKED
+        for i in range(19):
+            kept = field[i, x, pl.ds(8 * t, 8), :]
+            field[i, x, pl.ds(8 * t, 8), :] = jnp.where(fluid, f[i], kept)
+
+    odd = lax.rem(me_x, 2) == 1
+
+    for phase in range(ITERS):
         if phase == 0:
+            wait_rows()
+        else:
+            arrive(phase - 1)
+        edge_rows(phase)
+        x_up, x_down = x_copies(phase)
+        if phase == 0:
+            load_solid.wait()
+            load(0, 2, 4).wait()
+            plane(phase, rows - 1)
+            plane(phase, 0)
             pl.semaphore_wait(barrier, len(around))
         start(corner_copies(phase))
-        start(y_copies(phase))
+
+        @pl.when(odd)
+        def _():
+            if phase:
+                plane(phase, rows - 1)
+            x_up.start()
+            start(y_copies(phase))
+            if phase:
+                plane(phase, 0)
+            x_down.start()
+
+        @pl.when(jnp.logical_not(odd))
+        def _():
+            start(y_copies(phase))
+            if phase:
+                plane(phase, 0)
+            x_down.start()
+            if phase:
+                plane(phase, rows - 1)
+            x_up.start()
+
         if phase == 0:
-            load_solid.wait()
-            for copy in ends:
-                copy.wait()
-        plane(phase, rows - 1)
-        plane(phase, 0)
-        start(x_copies(phase))
-        if phase == 0:
-            for copy in inner:
-                copy.wait()
+            load(1, rows - 2, 5).wait()
 
         def step(x, carry):
             plane(phase, x)
@@ -269,34 +305,62 @@
 
         lax.fori_loop(1, rows - 1, step, 0)
 
-    last = ITERS - 1
-    for copy in x_copies(last) + y_copies(last) + corner_copies(last):
-        copy.wait_recv()
-    for phase in range(ITERS):
-        for copy in x_copies(phase) + y_copies(phase) + corner_copies(phase):
-            copy.wait_send()
+    def finish_step(c, carry):
+        for dx in range(2):
+            for t in range(1, tiles - 1):
+                finish(1 + 2 * c + dx, t)
+        return carry
+
+    lax.fori_loop(0, pairs, finish_step, 0)
+
+    view = flat[0].at[pl.ds(0, ITERS), pl.ds(0, sent)]
+    remote(view, view, 0, 1, 0).wait_send()
+    arrive(ITERS - 1)
 
 
 def finish_kernel(buf, field, out, stage, sem):
-    count, rows, cols, _ = stage.shape
-
-    def copy(x):
-        return pltpu.make_async_copy(stage.at[:, x], out.at[:, x], sem.at[x])
-
-    def step(x, carry):
-        for t in range(cols // 8):
-            load = tile_load(buf, x, t)
-            f = pull(load)
-            fluid = f[0] < BLOCKED
-            for i in range(count):
-                kept = field[i, x, pl.ds(8 * t, 8), :]
-                stage[i, x, pl.ds(8 * t, 8), :] = jnp.where(fluid, f[i], kept)
-        copy(x).start()
+    count, rows, cols, _ = out.shape
+    tiles = cols // 8
+    pairs = rows // 2
+    inside = pl.ds(8, cols - 16)
+    edges = (0, tiles - 1)
+
+    def inner_copy(c):
+        where = (slice(None), pl.ds(1 + 2 * c, 2), inside)
+        return pltpu.make_async_copy(field.at[where], out.at[where], sem.at[0])
+
+    def edge_copy(c, k):
+        where = (slice(None), pl.ds(2 * c, 2), pl.ds(8 * edges[k], 8))
+        return pltpu.make_async_copy(stage.at[where], out.at[where], sem.at[0])
+
+    def end_copy(x, k):
+        where = (slice(None), x, inside)
+        return pltpu.make_async_copy(stage.at[where], out.at[where], sem.at[0])
+
+    def finish(x, t):
+        f = pull(tile_load(buf, x, t))
+        fluid = f[0] < BLOCKED
+        for i in range(count):
+            kept = field[i, x, pl.ds(8 * t, 8), :]
+            stage[i, x, pl.ds(8 * t, 8), :] = jnp.where(fluid, f[i], kept)
+
+    for c in range(pairs - 1):
+        inner_copy(c).start()
+    for k, x in enumerate((0, rows - 1)):
+        for t in range(1, tiles - 1):
+            finish(x, t)
+        end_copy(x, k).start()
+
+    def step(c, carry):
+        for dx in range(2):
+            for t in edges:
+                finish(2 * c + dx, t)
+        for k in range(2):
+            edge_copy(c, k).start()
         return carry
 
-    lax.fori_loop(0, rows, step, 0)
-    for x in range(rows):
-        copy(x).wait()
+    lax.fori_loop(0, pairs, step, 0)
+    pltpu.make_async_copy(stage.at[:, pl.ds(0, rows), pl.ds(0, cols)], out, sem.at[0]).wait()
 
 
 def solution(mesh):
@@ -307,13 +371,14 @@
         count, rows, cols, lanes = populations.shape
         f32 = jnp.float32
         padded = (count, rows + 3, cols + PAD, lanes)
+        spaced = (count, rows + 1, cols + PAD, lanes)
         vmem = pl.BlockSpec(memory_space=pltpu.VMEM)
         hbm = pl.BlockSpec(memory_space=pltpu.HBM)
         post, field = pl.pallas_call(
             functools.partial(step_kernel, (rows, cols, gx_size, gy_size), (gx, gy)),
             out_shape=(
                 jax.ShapeDtypeStruct(padded, f32),
-                jax.ShapeDtypeStruct(populations.shape, f32),
+                jax.ShapeDtypeStruct(spaced, f32),
             ),
             in_specs=[hbm, hbm],
             out_specs=(vmem, vmem),
@@ -324,9 +389,9 @@
                 pltpu.VMEM((2, count, rows, lanes), f32),
                 pltpu.VMEM((2, rows, lanes), jnp.int32),
                 pltpu.VMEM((ITERS, 2, 5, rows, lanes), f32),
-                pltpu.SemaphoreType.DMA((7 + (rows - 2) // 2,)),
-                pltpu.SemaphoreType.DMA((ITERS, 9)),
-                pltpu.SemaphoreType.DMA((ITERS, 9)),
+                pltpu.SemaphoreType.DMA((6,)),
+                pltpu.SemaphoreType.DMA((1,)),
+                pltpu.SemaphoreType.DMA((ITERS,)),
             ],
             compiler_params=pltpu.CompilerParams(
                 collective_id=0, has_side_effects=True, vmem_limit_bytes=30 * 1024 * 1024
@@ -341,8 +406,8 @@
             in_specs=[vmem, vmem],
             out_specs=hbm,
             scratch_shapes=[
-                pltpu.VMEM(populations.shape, f32),
-                pltpu.SemaphoreType.DMA((rows,)),
+                pltpu.VMEM(spaced, f32),
+                pltpu.SemaphoreType.DMA((1,)),
             ],
             compiler_params=pltpu.CompilerParams(vmem_limit_bytes=12 * 1024 * 1024),
         )(post, field)

time: 22.7 us -> 21.5 us (0.947)
  Pallas kernels: 22.6 us -> 21.4 us
    pallas_call x1, Pallas kernels: 19.8 us -> 19.1 us  [local(): pl.pallas_call(functools.partial(step_kernel, (rows, cols, gx_size, gy_si...]
    pallas_call x1, Pallas kernels: 2.76 us -> 2.24 us  [local(): pl.pallas_call(finish_kernel, out_shape=jax.ShapeDtypeStruct(populations....]
where the time goes in v2:
time: 21.5 us; the launch traced here: 21.4 us
  Pallas kernels  21.4 us (100%)
    pallas_call x1, Pallas kernels, local(): pl.pallas_call(functools.partial(step_kernel, (rows, cols, gx_size, gy_si...  19.1 us
    pallas_call x1, Pallas kernels, local(): pl.pallas_call(finish_kernel, out_shape=jax.ShapeDtypeStruct(populations....  2.24 us

profile of v2, /device:TPU:0, one launch (start us, length us, event | category | flops | bytes accessed | tf_op | source)
XLA Modules:
  0.0 21.4 jit_solution(968358240587545919)
XLA Ops:
  0.0 19.1 %shard_map.28 = (f32[19,19,40,128]{3,2,1,0:T(8,128)S(1)}, f32[19,17,40,128]{3,2,1,0:T(8,128)S(1)}) custom-call(f32[19,16,32,128]{3,2,1,0:T(8,128)} %f_hbm.1, s32[16,32,128]{2,1,0:T(8,128)} %solid_hbm.1), custom_call_target="tpu_custom_call" | custom-call | tf_op jit(solution)/shard_map/pallas_call | solution.py:377
  19.1 2.2 %shard_map.29 = f32[19,16,32,128]{3,2,1,0:T(8,128)} custom-call(f32[19,19,40,128]{3,2,1,0:T(8,128)S(1)} %get-tuple-element.7.buf, f32[19,17,40,128]{3,2,1,0:T(8,128)S(1)} %get-tuple-element.8.field), custom_call_target="tpu_custom_call" | custom-call | tf_op jit(solution)/shard_map/pallas_call | solution.py:403

commit v3 on v2

--- a/solution.py
+++ b/solution.py
@@ -276,26 +276,13 @@
             pl.semaphore_wait(barrier, len(around))
         start(corner_copies(phase))
 
-        @pl.when(odd)
-        def _():
-            if phase:
-                plane(phase, rows - 1)
-            x_up.start()
-            start(y_copies(phase))
-            if phase:
-                plane(phase, 0)
-            x_down.start()
-
-        @pl.when(jnp.logical_not(odd))
-        def _():
-            start(y_copies(phase))
-            if phase:
-                plane(phase, 0)
-            x_down.start()
-            if phase:
-                plane(phase, rows - 1)
-            x_up.start()
-
+        start(y_copies(phase))
+        if phase:
+            plane(phase, rows - 1)
+        x_up.start()
+        if phase:
+            plane(phase, 0)
+        x_down.start()
         if phase == 0:
             load(1, rows - 2, 5).wait()
 

time: 21.5 us -> 21.4 us (level)
  no operation moved by 1% of the time
where the time goes in v3:
time: 21.4 us; the launch traced here: 21.2 us
  Pallas kernels  21.2 us (99%)
    pallas_call x1, Pallas kernels, local(): pl.pallas_call(functools.partial(step_kernel, (rows, cols, gx_size, gy_si...  19 us
    pallas_call x1, Pallas kernels, local(): pl.pallas_call(finish_kernel, out_shape=jax.ShapeDtypeStruct(populations....  2.24 us

profile of v3, /device:TPU:0, one launch (start us, length us, event | category | flops | bytes accessed | tf_op | source)
XLA Modules:
  0.0 21.2 jit_solution(1710702547475612325)
XLA Ops:
  0.0 19.0 %shard_map.28 = (f32[19,19,40,128]{3,2,1,0:T(8,128)S(1)}, f32[19,17,40,128]{3,2,1,0:T(8,128)S(1)}) custom-call(f32[19,16,32,128]{3,2,1,0:T(8,128)} %f_hbm.1, s32[16,32,128]{2,1,0:T(8,128)} %solid_hbm.1), custom_call_target="tpu_custom_call" | custom-call | tf_op jit(solution)/shard_map/pallas_call | solution.py:364
  19.0 2.2 %shard_map.29 = f32[19,16,32,128]{3,2,1,0:T(8,128)} custom-call(f32[19,19,40,128]{3,2,1,0:T(8,128)S(1)} %get-tuple-element.7.buf, f32[19,17,40,128]{3,2,1,0:T(8,128)S(1)} %get-tuple-element.8.field), custom_call_target="tpu_custom_call" | custom-call | tf_op jit(solution)/shard_map/pallas_call | solution.py:390

commit v4 on v3

--- a/solution.py
+++ b/solution.py
@@ -181,12 +181,12 @@
 
     def x_copies(phase):
         buf = buffers[phase]
-        own = pl.ds(PAD, cols)
         up, down = pl.ds(0, 5), pl.ds(8, 5)
-        return [
-            remote(buf.at[up, rows, own], buf.at[up, 0, own], phase, 1, 0),
-            remote(buf.at[down, 1, own], buf.at[down, rows + 1, own], phase, -1, 0),
-        ]
+        halves = [pl.ds(PAD + h * (cols // 2), cols // 2) for h in range(2)]
+        return (
+            [remote(buf.at[up, rows, own], buf.at[up, 0, own], phase, 1, 0) for own in halves],
+            [remote(buf.at[down, 1, own], buf.at[down, rows + 1, own], phase, -1, 0) for own in halves],
+        )
 
     def corner_copies(phase):
         buf = buffers[phase]
@@ -259,7 +259,6 @@
             kept = field[i, x, pl.ds(8 * t, 8), :]
             field[i, x, pl.ds(8 * t, 8), :] = jnp.where(fluid, f[i], kept)
 
-    odd = lax.rem(me_x, 2) == 1
 
     for phase in range(ITERS):
         if phase == 0:
@@ -277,12 +276,12 @@
         start(corner_copies(phase))
 
         start(y_copies(phase))
-        if phase:
-            plane(phase, rows - 1)
-        x_up.start()
-        if phase:
-            plane(phase, 0)
-        x_down.start()
+        for x, copies in ((rows - 1, x_up), (0, x_down)):
+            for h, copy in enumerate(copies):
+                if phase:
+                    for t in range(h * tiles // 2, (h + 1) * tiles // 2):
+                        advance(phase, x, t)
+                copy.start()
         if phase == 0:
             load(1, rows - 2, 5).wait()
 

time: 21.4 us -> 21.3 us (level)
  no operation moved by 1% of the time
where the time goes in v4:
time: 21.3 us; the launch traced here: 21.1 us
  Pallas kernels  21.1 us (99%)
    pallas_call x1, Pallas kernels, local(): pl.pallas_call(functools.partial(step_kernel, (rows, cols, gx_size, gy_si...  18.9 us
    pallas_call x1, Pallas kernels, local(): pl.pallas_call(finish_kernel, out_shape=jax.ShapeDtypeStruct(populations....  2.24 us

profile of v4, /device:TPU:0, one launch (start us, length us, event | category | flops | bytes accessed | tf_op | source)
XLA Modules:
  0.0 21.1 jit_solution(11496200203679019623)
XLA Ops:
  0.0 18.9 %shard_map.28 = (f32[19,19,40,128]{3,2,1,0:T(8,128)S(1)}, f32[19,17,40,128]{3,2,1,0:T(8,128)S(1)}) custom-call(f32[19,16,32,128]{3,2,1,0:T(8,128)} %f_hbm.1, s32[16,32,128]{2,1,0:T(8,128)} %solid_hbm.1), custom_call_target="tpu_custom_call" | custom-call | tf_op jit(solution)/shard_map/pallas_call | solution.py:363
  18.9 2.2 %shard_map.29 = f32[19,16,32,128]{3,2,1,0:T(8,128)} custom-call(f32[19,19,40,128]{3,2,1,0:T(8,128)S(1)} %get-tuple-element.7.buf, f32[19,17,40,128]{3,2,1,0:T(8,128)S(1)} %get-tuple-element.8.field), custom_call_target="tpu_custom_call" | custom-call | tf_op jit(solution)/shard_map/pallas_call | solution.py:389

commit v5 on v4

--- a/solution.py
+++ b/solution.py
@@ -169,23 +169,23 @@
         row_loads[1].wait()
         row_loads[3].wait()
 
-    def remote(src, dst, phase, dx, dy):
+    def remote(src, dst, phase, dx, dy, kind=0):
         return pltpu.make_async_remote_copy(
             src_ref=src,
             dst_ref=dst,
             send_sem=send_sem.at[0],
-            recv_sem=recv_sem.at[phase],
+            recv_sem=recv_sem.at[phase, kind],
             device_id=device(dx, dy),
             device_id_type=MESH,
         )
 
-    def x_copies(phase):
+    def x_copies(phase, spans):
         buf = buffers[phase]
         up, down = pl.ds(0, 5), pl.ds(8, 5)
-        halves = [pl.ds(PAD + h * (cols // 2), cols // 2) for h in range(2)]
+        spans = [pl.ds(PAD + 8 * first, 8 * count) for first, count in spans]
         return (
-            [remote(buf.at[up, rows, own], buf.at[up, 0, own], phase, 1, 0) for own in halves],
-            [remote(buf.at[down, 1, own], buf.at[down, rows + 1, own], phase, -1, 0) for own in halves],
+            [remote(buf.at[up, rows, own], buf.at[up, 0, own], phase, 1, 0, 1) for own in spans],
+            [remote(buf.at[down, 1, own], buf.at[down, rows + 1, own], phase, -1, 0, 1) for own in spans],
         )
 
     def corner_copies(phase):
@@ -208,9 +208,10 @@
             remote(y_send.at[phase, 1, 4], buf.at[0, pl.ds(2, rows), 0], phase, 0, -1),
         ]
 
-    def arrive(phase):
-        view = flat[phase].at[0, pl.ds(0, sent)]
-        remote(view, view, phase, 1, 0).wait_recv()
+    def arrive(phase, kind):
+        count = 10 * cols if kind else 10 * rows + len(CORNERS)
+        view = flat[phase].at[0, pl.ds(0, count)]
+        remote(view, view, phase, 1, 0, kind).wait_recv()
 
     def row(phase, side, g):
         fluid = s_row[side, pl.ds(8 * g, 8), :] == 0
@@ -260,13 +261,19 @@
             field[i, x, pl.ds(8 * t, 8), :] = jnp.where(fluid, f[i], kept)
 
 
+    middle, outer, whole = ((1, tiles - 2),), ((0, 1), (tiles - 1, 1)), ((0, tiles),)
+
     for phase in range(ITERS):
         if phase == 0:
             wait_rows()
         else:
-            arrive(phase - 1)
+            arrive(phase - 1, 1)
+            for x, copies in zip((rows - 1, 0), x_copies(phase, middle)):
+                for t in range(1, tiles - 1):
+                    advance(phase, x, t)
+                start(copies)
+            arrive(phase - 1, 0)
         edge_rows(phase)
-        x_up, x_down = x_copies(phase)
         if phase == 0:
             load_solid.wait()
             load(0, 2, 4).wait()
@@ -276,12 +283,12 @@
         start(corner_copies(phase))
 
         start(y_copies(phase))
-        for x, copies in ((rows - 1, x_up), (0, x_down)):
-            for h, copy in enumerate(copies):
-                if phase:
-                    for t in range(h * tiles // 2, (h + 1) * tiles // 2):
-                        advance(phase, x, t)
-                copy.start()
+        for x, copies in zip((rows - 1, 0), x_copies(phase, outer if phase else whole)):
+            if phase:
+                for t in (0, tiles - 1):
+                    advance(phase, x, t)
+            start(copies)
+
         if phase == 0:
             load(1, rows - 2, 5).wait()
 
@@ -301,7 +308,8 @@
 
     view = flat[0].at[pl.ds(0, ITERS), pl.ds(0, sent)]
     remote(view, view, 0, 1, 0).wait_send()
-    arrive(ITERS - 1)
+    arrive(ITERS - 1, 1)
+    arrive(ITERS - 1, 0)
 
 
 def finish_kernel(buf, field, out, stage, sem):
@@ -377,7 +385,7 @@
                 pltpu.VMEM((ITERS, 2, 5, rows, lanes), f32),
                 pltpu.SemaphoreType.DMA((6,)),
                 pltpu.SemaphoreType.DMA((1,)),
-                pltpu.SemaphoreType.DMA((ITERS,)),
+                pltpu.SemaphoreType.DMA((ITERS, 2)),
             ],
             compiler_params=pltpu.CompilerParams(
                 collective_id=0, has_side_effects=True, vmem_limit_bytes=30 * 1024 * 1024

time: 21.3 us -> 21.3 us (level)
  no operation moved by 1% of the time
where the time goes in v5:
time: 21.3 us; the launch traced here: 21.2 us
  Pallas kernels  21.2 us (100%)
    pallas_call x1, Pallas kernels, local(): pl.pallas_call(functools.partial(step_kernel, (rows, cols, gx_size, gy_si...  18.9 us
    pallas_call x1, Pallas kernels, local(): pl.pallas_call(finish_kernel, out_shape=jax.ShapeDtypeStruct(populations....  2.24 us

profile of v5, /device:TPU:0, one launch (start us, length us, event | category | flops | bytes accessed | tf_op | source)
XLA Modules:
  0.0 21.2 jit_solution(13757422045497037141)
XLA Ops:
  0.0 18.9 %shard_map.28 = (f32[19,19,40,128]{3,2,1,0:T(8,128)S(1)}, f32[19,17,40,128]{3,2,1,0:T(8,128)S(1)}) custom-call(f32[19,16,32,128]{3,2,1,0:T(8,128)} %f_hbm.1, s32[16,32,128]{2,1,0:T(8,128)} %solid_hbm.1), custom_call_target="tpu_custom_call" | custom-call | tf_op jit(solution)/shard_map/pallas_call | solution.py:371
  18.9 2.2 %shard_map.29 = f32[19,16,32,128]{3,2,1,0:T(8,128)} custom-call(f32[19,19,40,128]{3,2,1,0:T(8,128)S(1)} %get-tuple-element.7.buf, f32[19,17,40,128]{3,2,1,0:T(8,128)S(1)} %get-tuple-element.8.field), custom_call_target="tpu_custom_call" | custom-call | tf_op jit(solution)/shard_map/pallas_call | solution.py:397
